TPU v7x, 32 devices: a whole 2x2x4 slice. The times are simulated.
32 devices in a mesh: dp: 8 (over y, x, core), mp: 4 (over z).
Axes of the slice: x: 2, y: 2, z: 4, core: 2. Of those that a mesh axis runs over, the one named last changes fastest.
Arguments:
- tokens: bfloat16 [16384, 1024], P(('dp', 'mp')), may hold values from -6 to 6
- norm_gain: float32 [2, 1024], replicated, may hold values from 0.1 to 1.9
- qkv_weight: bfloat16 [3, 1024, 1024], P(None, 'dp', 'mp')
- out_weight: bfloat16 [1024, 1024], P('mp', 'dp'), may hold values from -0.1875 to 0.1875
- variate_bias: float32 [2, 16], replicated, may hold values from -6 to 6
- ffn_weight: bfloat16 [2, 1024, 2816], P(None, 'dp', 'mp'), may hold values from -0.1875 to 0.1875
- down_weight: bfloat16 [2816, 1024], P('mp', 'dp'), may hold values from -0.109375 to 0.109375
- sample_ids: int32 [16384], P(('dp', 'mp')), may hold values from 0 to 127, as said below
- variate_ids: int32 [16384], P(('dp', 'mp')), may hold values from 0 to 15, as said below
- time_ids: int32 [16384], P(('dp', 'mp')), may hold values from 0 to 31, as said below
Outputs:
- encoded: bfloat16 [16384, 1024], P(('dp', 'mp'))
Inputs may be any that keep to these rules, and one draw needn't show every extreme that they name: `sample_ids`: within each packed sequence of 512 tokens the series numbers start at 0 and never fall; a series with v variates (1 to 16) and p patches (4 to 32) holds v * p consecutive tokens, the last series of a sequence may be cut short; some packed sequence holds 128 series of one variate and four patches each. `variate_ids`: A token's offset within its series divided by that series' patch count p. `time_ids`: A token's offset within its series modulo that series' patch count p.
All inputs are finite; a program needn't handle non-finite values.
Results may differ from a plain program's by a relative error of at most 0.017.
Values may be sent and summed in bfloat16 or wider, within the bound.
A program may use at most 128 MiB of HBM per device.

v0:
```python
import jax
import jax.numpy as jnp
from jax import lax
from jax.sharding import PartitionSpec as P

HEAD_DIM = 64
L = 512


def rms_norm(values, gain):
    wide = values.astype(jnp.float32)
    square = jnp.mean(wide * wide, axis=-1, keepdims=True)
    return (wide * lax.rsqrt(square + 1e-05) * gain[None, :]).astype(jnp.bfloat16)


def rotate(values, times):
    half = values.shape[-1] // 2
    freq = 10000.0 ** (-jnp.arange(half, dtype=jnp.float32) / half)
    angle = times.astype(jnp.float32)[:, None] * freq[None, :]
    cosine = jnp.cos(angle)[:, None, :]
    sine = jnp.sin(angle)[:, None, :]
    first = values[..., :half]
    second = values[..., half:]
    return jnp.concatenate(
        [first * cosine - second * sine, first * sine + second * cosine], axis=-1
    )


def rotated(raw, times):
    row_total, local_width = raw.shape
    turned = rotate(raw.reshape(row_total, local_width // HEAD_DIM, HEAD_DIM), times)
    return turned.reshape(row_total, local_width).astype(jnp.bfloat16)


def attend(queries, keys_rot, values, samples, variates, bias):
    row_total, local_width = queries.shape
    heads_here = local_width // HEAD_DIM
    count = row_total // L

    def one_sequence(args):
        qs, ks, vs, sample_row, variate_row = args
        scores = jnp.einsum(
            "qhd,khd->hqk", qs, ks, preferred_element_type=jnp.float32
        ) * HEAD_DIM ** (-0.5)
        same = variate_row[:, None] == variate_row[None, :]
        scores = scores + jnp.where(same[None], bias[0][:, None, None], bias[1][:, None, None])
        scores = jnp.where((sample_row[:, None] == sample_row[None, :])[None], scores, -1e30)
        top = jnp.max(scores, axis=2, keepdims=True)
        expo = jnp.exp(scores - top)
        weights = (expo / jnp.sum(expo, axis=2, keepdims=True)).astype(jnp.bfloat16)
        return jnp.einsum("hqk,khd->qhd", weights, vs, preferred_element_type=jnp.float32).astype(
            jnp.bfloat16
        )

    shape = (count, L, heads_here, HEAD_DIM)
    result = lax.map(
        one_sequence,
        (
            queries.reshape(shape),
            keys_rot.reshape(shape),
            values.reshape(shape),
            samples.reshape(count, L),
            variates.reshape(count, L),
        ),
    )
    return result.reshape(row_total, local_width)


def local(
    tokens,
    norm_gain,
    qkv_weight,
    out_weight,
    variate_bias,
    ffn_weight,
    down_weight,
    sample_ids,
    variate_ids,
    time_ids,
):
    heads_here = qkv_weight.shape[2] // HEAD_DIM
    head_start = lax.axis_index("mp") * heads_here
    bias_local = lax.dynamic_slice_in_dim(variate_bias, head_start, heads_here, 1)
    first_normed = rms_norm(tokens, norm_gain[0])
    wide_columns = lax.all_gather(qkv_weight, "mp", axis=2, tiled=True)
    columns = first_normed
    projected = jnp.einsum(
        "rc,jcd->jrd",
        columns,
        lax.all_gather(wide_columns, "dp", axis=1, tiled=True),
        preferred_element_type=jnp.float32,
    )
    queries = rotated(projected[0], time_ids)
    keys_rot = rotated(projected[1], time_ids)
    values = projected[2].astype(jnp.bfloat16)
    grouped = lax.all_to_all(
        jnp.stack([queries, keys_rot, values]), "mp", split_axis=2, concat_axis=1, tiled=True
    )
    gathered_ids = (
        lax.all_gather(sample_ids, "mp", axis=0, tiled=True),
        lax.all_gather(variate_ids, "mp", axis=0, tiled=True),
    )
    attended = attend(
        grouped[0], grouped[1], grouped[2], gathered_ids[0], gathered_ids[1], bias_local
    )
    back_rows = lax.all_to_all(attended, "mp", split_axis=0, concat_axis=1, tiled=True)
    out_rows = lax.all_gather(out_weight, "mp", axis=0, tiled=True)
    mixed = jnp.dot(
        back_rows,
        lax.all_gather(out_rows, "dp", axis=1, tiled=True),
        preferred_element_type=jnp.float32,
    )
    residual = (tokens.astype(jnp.float32) + mixed).astype(jnp.bfloat16)
    second_normed = rms_norm(residual, norm_gain[1])
    ffn_columns = lax.all_gather(ffn_weight, "mp", axis=2, tiled=True)
    columns = second_normed
    gate_up = jnp.einsum(
        "rc,jcf->jrf",
        columns,
        lax.all_gather(ffn_columns, "dp", axis=1, tiled=True),
        preferred_element_type=jnp.float32,
    )
    hidden = (jax.nn.silu(gate_up[0]) * gate_up[1]).astype(jnp.bfloat16)
    down_full = lax.all_gather(down_weight, "mp", axis=0, tiled=True)
    feed = jnp.dot(
        hidden,
        lax.all_gather(down_full, "dp", axis=1, tiled=True),
        preferred_element_type=jnp.float32,
    )
    return (residual.astype(jnp.float32) + feed).astype(jnp.bfloat16)


def solution(mesh):
    return jax.shard_map(
        local,
        mesh=mesh,
        in_specs=(
            P(("dp", "mp"), None),
            P(),
            P(None, "dp", "mp"),
            P("mp", "dp"),
            P(),
            P(None, "dp", "mp"),
            P("mp", "dp"),
            P(("dp", "mp")),
            P(("dp", "mp")),
            P(("dp", "mp")),
        ),
        out_specs=P(("dp", "mp"), None),
        check_vma=False,
    )
```

profile of v0, /device:TPU:0, one launch (start us, length us, event | category | flops | bytes accessed | tf_op | source)
XLA Modules:
  0.0 358.3 jit_solution(14907393396261247635)
XLA Ops:
  6.5 2.2 copy.40
  8.8 27.7 %all_gather.30 = bf16[3,128,1024]{2,1,0:T(8,128)(2,1)} all-gather(bf16[3,128,256]{2,1,0:T(8,128)(2,1)} %param.14), channel_id=1, replica_groups=mesh['dp'=8,'mp'=4] {'mp'}, dimensions={2}, use_global_device_ids=true | all-gather | bytes 983040 | tf_op jit(solution)/shard_map/all_gather | solution.py:85
  36.6 18.9 %all_gather.34 = bf16[1024,128]{1,0:T(8,128)(2,1)} all-gather(bf16[256,128]{1,0:T(8,128)(2,1)} %param.15), channel_id=1, replica_groups=mesh['dp'=8,'mp'=4] {'mp'}, dimensions={0}, use_global_device_ids=true | all-gather | bytes 327680 | tf_op jit(solution)/shard_map/all_gather | solution.py:107
  55.5 1.2 all-gather.12.cloned.1.call-done
  56.8 4.9 %copy.41 = bf16[2,128,2816]{2,1,0:T(8,128)(2,1)} copy(bf16[2,128,2816]{1,0,2:T(2,128)(2,1)} %all-gather.12.cloned.1.call-done) | data formatting | bytes 2883584 | tf_op jit(solution)/shard_map/all_gather | solution.py:115
  61.7 0.3 fusion.56
  62.0 0.3 multiply_cosine_fusion
  62.3 41.2 %all-gather.8.cloned.1.call-done = bf16[3,1024,1024]{2,1,0:T(8,128)(2,1)} async-done(((bf16[3,128,1024]{2,1,0:T(8,128)(2,1)}), bf16[3,1024,1024]{2,1,0:T(8,128)(2,1)}) %all-gather.8.cloned.1.call-update) | async-done | bytes 6291472 | tf_op jit(solution)/shard_map/all_gather | solution.py:90
  103.5 5.7 %convolution_bitcast_fusion.1 = f32[3,512,1024]{2,1,0:T(8,128)S(1)} fusion(bf16[3,1024,1024]{2,1,0:T(8,128)(2,1)} %all-gather.8.cloned.1.call-done, bf16[512,1024]{1,0:T(8,128)(2,1)S(1)} %copy-done.2, f32[1024]{0:T(1024)S(1)} %bitcast.128, f32[512]{0:T(512)S(1)} %add_rsqrt_fusion.1), kind=kOutput, calls=%fused_computation.54 | convolution fusion | flops 3223322624 | bytes 13637632 | tf_op jit(solution)/shard_map/rc,jcd->jrd/dot_general | solution.py:87
  109.3 1.1 slice.103
  110.4 2.4 fusion.80
  112.8 2.0 copy.34
  114.8 2.9 copy.35
  117.7 2.3 subtract_convert_fusion.1
  120.0 0.1 pad_maximum_fusion.1
  120.1 1.3 copy.36
  121.5 1.3 copy.37
  122.8 2.5 pad_maximum_fusion
  125.3 5.7 %copy.38 = bf16[3,512,1024]{1,0,2:T(4,128)(2,1)} copy(bf16[3,512,1024]{2,1,0:T(8,128)(2,1)S(1)} %pad_maximum_fusion) | data formatting | bytes 6291456 | tf_op jit(solution)/shard_map/stack | solution.py:97
  131.0 5.0 %all-to-all-start = ((bf16[3,512,1024]{1,0,2:T(4,128)(2,1)}), bf16[3,512,1024]{1,0,2:T(4,128)(2,1)}, u32[]{:S(2)}, u32[]{:S(2)}) async-start(bf16[3,512,1024]{1,0,2:T(4,128)(2,1)} %copy.38), calls=%async_computation | async-start | bytes 8388608 | tf_op jit(solution)/shard_map/all_to_all | solution.py:96
  136.1 106.7 %all_gather.38 = bf16[2816,128]{1,0:T(8,128)(2,1)} all-gather(bf16[704,128]{1,0:T(8,128)(2,1)S(1)} %copy-done.4), channel_id=1, replica_groups=mesh['dp'=8,'mp'=4] {'mp'}, dimensions={0}, use_global_device_ids=true | all-gather | bytes 901120 | tf_op jit(solution)/shard_map/all_gather | solution.py:124
  242.9 11.9 %all-gather.1 = s32[4,1,512]{2,1,0:T(1,128)S(1)} all-gather(s32[1,1,512]{2,1,0:T(1,128)S(1)} %bitcast.129), channel_id=1, replica_groups=mesh['dp'=8,'mp'=4] {'mp'}, dimensions={0}, use_global_device_ids=true | all-gather | bytes 10240 | tf_op jit(solution)/shard_map/all_gather | solution.py:101
  254.8 12.1 %all-gather = s32[4,1,512]{2,1,0:T(1,128)S(1)} all-gather(s32[1,1,512]{2,1,0:T(1,128)S(1)} %bitcast.130), channel_id=1, replica_groups=mesh['dp'=8,'mp'=4] {'mp'}, dimensions={0}, use_global_device_ids=true | all-gather | bytes 10240 | tf_op jit(solution)/shard_map/all_gather | solution.py:100
  266.9 0.1 constant_dynamic-slice_fusion.2
  267.0 3.2 copy.39
  270.2 1.5 fusion.81
  271.7 31.2 %while.10 = (s32[]{:T(128)}, bf16[4,512,4,64]{1,3,2,0:T(8,128)(2,1)}, bf16[4,512,4,64]{1,3,2,0:T(8,128)(2,1)}, s32[4,512]{1,0:T(4,128)S(1)}, bf16[4,512,4,64]{1,...) while((s32[]{:T(128)}, ...), condition=%wide.region_4.5_spmd, body=%wide.region_1.4_spmd.sunk | while | flops 416943104 | bytes 3179681 | solution.py:56
  271.7 0.2 broadcast_compare_fusion.4
  271.9 0.2 broadcast_compare_fusion.5
  272.2 3.0 fusion.100
  275.2 4.3 %fusion.101 = bf16[4,512,4,64]{1,3,2,0:T(8,128)(2,1)} fusion(bf16[4,512,4,64]{1,3,2,0:T(8,128)(2,1)} %get-tuple-element.154, s32[]{:T(128)} %get-tuple-element.153, f32[4,512]{1,0:T(4,128)S(1)} %fusion.100, bf16[4,512,4,64]{1,3,2,0:T(8,128)(2,1)} %get-tuple-element.164, f32[4]{0:T(128)S(1)} %get-tuple-element.140, f32[4]{0:T(128)S(1)} %get-tuple-element.141, ...), kind=kOutput, calls=%fused_computation.14.clone.1 | convolution fusion | flops 275909120 | bytes 1584128 | tf_op jit(solution)/shard_map/while/body/eval_jaxpr/hqk,khd->qhd/dot_general | solution.py:51
  279.5 0.2 broadcast_compare_fusion.4
  279.7 0.2 broadcast_compare_fusion.5
  280.0 3.0 fusion.100
  283.0 4.3 %fusion.101 = bf16[4,512,4,64]{1,3,2,0:T(8,128)(2,1)} fusion(bf16[4,512,4,64]{1,3,2,0:T(8,128)(2,1)} %get-tuple-element.154, s32[]{:T(128)} %get-tuple-element.153, f32[4,512]{1,0:T(4,128)S(1)} %fusion.100, bf16[4,512,4,64]{1,3,2,0:T(8,128)(2,1)} %get-tuple-element.164, f32[4]{0:T(128)S(1)} %get-tuple-element.140, f32[4]{0:T(128)S(1)} %get-tuple-element.141, ...), kind=kOutput, calls=%fused_computation.14.clone.1 | convolution fusion | flops 275909120 | bytes 1584128 | tf_op jit(solution)/shard_map/while/body/eval_jaxpr/hqk,khd->qhd/dot_general | solution.py:51
  287.3 0.2 broadcast_compare_fusion.4
  287.5 0.2 broadcast_compare_fusion.5
  287.8 3.0 fusion.100
  290.8 4.3 %fusion.101 = bf16[4,512,4,64]{1,3,2,0:T(8,128)(2,1)} fusion(bf16[4,512,4,64]{1,3,2,0:T(8,128)(2,1)} %get-tuple-element.154, s32[]{:T(128)} %get-tuple-element.153, f32[4,512]{1,0:T(4,128)S(1)} %fusion.100, bf16[4,512,4,64]{1,3,2,0:T(8,128)(2,1)} %get-tuple-element.164, f32[4]{0:T(128)S(1)} %get-tuple-element.140, f32[4]{0:T(128)S(1)} %get-tuple-element.141, ...), kind=kOutput, calls=%fused_computation.14.clone.1 | convolution fusion | flops 275909120 | bytes 1584128 | tf_op jit(solution)/shard_map/while/body/eval_jaxpr/hqk,khd->qhd/dot_general | solution.py:51
  295.1 0.2 broadcast_compare_fusion.4
  295.4 0.2 broadcast_compare_fusion.5
  295.6 3.0 fusion.100
  298.6 4.3 %fusion.101 = bf16[4,512,4,64]{1,3,2,0:T(8,128)(2,1)} fusion(bf16[4,512,4,64]{1,3,2,0:T(8,128)(2,1)} %get-tuple-element.154, s32[]{:T(128)} %get-tuple-element.153, f32[4,512]{1,0:T(4,128)S(1)} %fusion.100, bf16[4,512,4,64]{1,3,2,0:T(8,128)(2,1)} %get-tuple-element.164, f32[4]{0:T(128)S(1)} %get-tuple-element.140, f32[4]{0:T(128)S(1)} %get-tuple-element.141, ...), kind=kOutput, calls=%fused_computation.14.clone.1 | convolution fusion | flops 275909120 | bytes 1584128 | tf_op jit(solution)/shard_map/while/body/eval_jaxpr/hqk,khd->qhd/dot_general | solution.py:51
  302.9 3.7 %all-to-all-start.1 = ((bf16[4,512,256]{1,2,0:T(8,128)(2,1)}), bf16[4,512,256]{1,2,0:T(8,128)(2,1)S(1)}, u32[]{:S(2)}, u32[]{:S(2)}) async-start(bf16[4,512,256]{1,2,0:T(8,128)(2,1)} %bitcast.24), calls=%async_computation.1 | async-start | bytes 2097152 | tf_op jit(solution)/shard_map/all_to_all | solution.py:106
  306.7 18.6 %all-to-all-done.1 = bf16[4,512,256]{1,2,0:T(8,128)(2,1)S(1)} async-done(((bf16[4,512,256]{1,2,0:T(8,128)(2,1)}), bf16[4,512,256]{1,2,0:T(8,128)(2,1)S(1)}, u32[]{:S(2)}, u32[]{:S(2)}) %all-to-all-start.1) | async-done | bytes 1048608 | tf_op jit(solution)/shard_map/all_to_all | solution.py:106
  325.3 3.0 fusion.60
  328.3 13.2 %convolution_bitcast_fusion = f32[2,512,2816]{2,1,0:T(8,128)} fusion(bf16[2,1024,2816]{2,1,0:T(8,128)(2,1)} %all-gather.14.cloned.1.call-done, bf16[512,1024]{1,0:T(8,128)(2,1)S(1)} %get-tuple-element.84, f32[1024]{0:T(1024)S(1)} %bitcast.125, f32[512]{0:T(512)S(1)} %add_rsqrt_fusion), kind=kOutput, calls=%fused_computation.41 | convolution fusion | flops 5907677184 | bytes 24123392 | tf_op jit(solution)/shard_map/rc,jcf->jrf/dot_general | solution.py:117
  341.6 10.2 %fusion.63 = bf16[512,1024]{1,0:T(8,128)(2,1)} fusion(bf16[512,1024]{1,0:T(8,128)(2,1)S(1)} %get-tuple-element.84, bf16[2816,1024]{1,0:T(8,128)(2,1)} %all-gather.16.cloned.1.call-done, f32[2,512,2816]{2,1,0:T(8,128)} %convolution_bitcast_fusion), kind=kOutput, calls=%fused_computation.62 | convolution fusion | flops 2963013632 | bytes 19398656 | tf_op jit(solution)/shard_map/dot_general | solution.py:125
  (48 shorter events, 0.4 us)
Async XLA Ops:
  6.5 260.4 %copy-start = (f32[2,16]{1,0:T(2,128)S(1)}, f32[2,16]{1,0:T(2,128)}, u32[]{:S(2)}) copy-start(f32[2,16]{1,0:T(2,128)} %param.16) | copy-start | bytes 388
  6.5 55.1 %copy-start.8 = (s32[512]{0:T(512)S(1)}, s32[512]{0:T(512)}, u32[]{:S(2)}) copy-start(s32[512]{0:T(512)} %param.21) | copy-start | bytes 6148
  6.5 55.2 %copy-start.2 = (bf16[512,1024]{1,0:T(8,128)(2,1)S(1)}, bf16[512,1024]{1,0:T(8,128)(2,1)}, u32[]{:S(2)}) copy-start(bf16[512,1024]{1,0:T(8,128)(2,1)} %param.12) | copy-start | bytes 3145732
  6.5 50.2 %all-gather.12.cloned.1.call-start = ((), (), s32[]{:S(2)}) async-start(), calls=%async_computation.4 | async-start | bytes 1802240 | tf_op jit(solution)/shard_map/all_gather | solution.py:115
  8.7 53.3 %copy-start.5 = (f32[2,1024]{1,0:T(2,128)S(1)}, f32[2,1024]{1,0:T(2,128)}, u32[]{:S(2)}) copy-start(f32[2,1024]{1,0:T(2,128)} %param.13) | copy-start | bytes 24580
  8.8 94.8 %all-gather.8.cloned.1.call-start = ((), (), s32[]{:S(2)}) async-start(), calls=%async_computation.2 | async-start | bytes 7077888 | tf_op jit(solution)/shard_map/all_gather | solution.py:90
  36.5 270.2 %all-gather.10.cloned.1.call-start = ((), (), s32[]{:S(2)}) async-start(), calls=%async_computation.3 | async-start | bytes 2359296 | tf_op jit(solution)/shard_map/all_gather | solution.py:110
  55.5 272.8 %all-gather.14.cloned.1.call-start = ((), (), s32[]{:S(2)}) async-start(), calls=%async_computation.5 | async-start | bytes 12976128 | tf_op jit(solution)/shard_map/all_gather | solution.py:120
  131.0 5.1 %copy-start.4 = (bf16[704,128]{1,0:T(8,128)(2,1)S(1)}, bf16[704,128]{1,0:T(8,128)(2,1)}, u32[]{:S(2)}) copy-start(bf16[704,128]{1,0:T(8,128)(2,1)} %param.18) | copy-start | bytes 540676
  131.0 111.8 %copy-start.6 = (s32[512]{0:T(512)S(1)}, s32[512]{0:T(512)}, u32[]{:S(2)}) copy-start(s32[512]{0:T(512)} %param.20) | copy-start | bytes 6148
  131.0 123.8 %copy-start.7 = (s32[512]{0:T(512)S(1)}, s32[512]{0:T(512)}, u32[]{:S(2)}) copy-start(s32[512]{0:T(512)} %param.19) | copy-start | bytes 6148
  131.0 136.0 %all-to-all-start = ((bf16[3,512,1024]{1,0,2:T(4,128)(2,1)}), bf16[3,512,1024]{1,0,2:T(4,128)(2,1)}, u32[]{:S(2)}, u32[]{:S(2)}) async-start(bf16[3,512,1024]{1,0,2:T(4,128)(2,1)} %copy.38), calls=%async_computation | async-start | bytes 8388608 | tf_op jit(solution)/shard_map/all_to_all | solution.py:96
  136.0 205.6 %all-gather.16.cloned.1.call-start = ((), (), s32[]{:S(2)}) async-start(), calls=%async_computation.6 | async-start | bytes 6488064 | tf_op jit(solution)/shard_map/all_gather | solution.py:127
  271.7 53.6 %copy-start.3 = (bf16[512,1024]{1,0:T(8,128)(2,1)S(1)}, bf16[512,1024]{1,0:T(8,128)(2,1)}, u32[]{:S(2)}) copy-start(bf16[512,1024]{1,0:T(8,128)(2,1)} %param.12) | copy-start | bytes 3145732
  302.9 22.3 %all-to-all-start.1 = ((bf16[4,512,256]{1,2,0:T(8,128)(2,1)}), bf16[4,512,256]{1,2,0:T(8,128)(2,1)S(1)}, u32[]{:S(2)}, u32[]{:S(2)}) async-start(bf16[4,512,256]{1,2,0:T(8,128)(2,1)} %bitcast.24), calls=%async_computation.1 | async-start | bytes 2097152 | tf_op jit(solution)/shard_map/all_to_all | solution.py:106
  341.6 10.2 %copy-start.1 = (f32[2,16]{1,0:T(2,128)S(1)}, f32[2,16]{1,0:T(2,128)}, u32[]{:S(2)}) copy-start(f32[2,16]{1,0:T(2,128)} %param.16) | copy-start | bytes 388
Sparse Core Ops, SparseCore 0:
  8.9 47.8 all-gather.11
  58.7 44.7 all-gather.7
  105.4 28.0 all-gather.9
  135.3 67.5 all-gather.13
  243.0 44.4 all-gather.15
where the time goes:
time: 359 us; the launch traced here: 358 us
  blocking collectives  177 us (49%)
  matrix products  61.5 us (17%)
  waiting for transfers between devices  61.1 us (17%)
  local copies, waits for them, and re-layouts  28.7 us (8%)
  between operations  13.3 us (4%)
  starting transfers between devices  8.9 us (2%)
  other arithmetic  7.24 us (2%)
    all_gather x1, blocking collectives, local(): down_full = lax.all_gather(down_weight, 'mp', axis=0, tiled=True)  107 us
    all_gather x1, waiting for transfers between devices, local(): lax.all_gather(wide_columns, 'dp', axis=1, tiled=True)  41.2 us
    all_gather x1, blocking collectives, local(): wide_columns = lax.all_gather(qkv_weight, 'mp', axis=2, tiled=True)  27.7 us
    all_gather x1, blocking collectives, local(): out_rows = lax.all_gather(out_weight, 'mp', axis=0, tiled=True)  18.9 us
    all_to_all x1, waiting for transfers between devices, local(): lax.all_to_all(attended, 'mp', split_axis=0, concat_axis=1, tiled=True)  18.6 us
    dot_general x4, matrix products, one_sequence(): jnp.einsum('hqk,khd->qhd', weights, vs, preferred_element_type=jnp.float32)  17.2 us
    dot_general x1, matrix products, local(): jnp.einsum('rc,jcf->jrf', columns, lax.all_gather(ffn_columns, 'dp', axis...  13.2 us
    sub x4, matrix products, one_sequence(): expo = jnp.exp(scores - top)  12.1 us
  transfers between devices with their start and end apart: 7, of which 3 were waited for; matrix products, arithmetic and copies ran while one was open for 24% of the time, Pallas kernels for 0%

commit v1 on v0

--- a/solution.py
+++ b/solution.py
@@ -1,3 +1,4 @@
+import functools
 import jax
 import jax.numpy as jnp
 from jax import lax
@@ -5,6 +6,15 @@
 
 HEAD_DIM = 64
 L = 512
+
+
+def results_raise(vec, mesh_name, d0):
+    frame_out = lax.all_gather(vec, mesh_name)
+    near = jnp.concatenate(frame_out, axis=d0)
+    return near
+
+
+clear_regions_for = functools.partial(results_raise, mesh_name="dp", d0=1)
 
 
 def rms_norm(values, gain):
@@ -122,11 +132,7 @@
     )
     hidden = (jax.nn.silu(gate_up[0]) * gate_up[1]).astype(jnp.bfloat16)
     down_full = lax.all_gather(down_weight, "mp", axis=0, tiled=True)
-    feed = jnp.dot(
-        hidden,
-        lax.all_gather(down_full, "dp", axis=1, tiled=True),
-        preferred_element_type=jnp.float32,
-    )
+    feed = jnp.dot(hidden, clear_regions_for(down_full), preferred_element_type=jnp.float32)
     return (residual.astype(jnp.float32) + feed).astype(jnp.bfloat16)
 
 

time: 359 us -> 336 us (0.936)
  waiting for transfers between devices: 61.1 us -> 38.3 us
  matrix products: 61.5 us -> 48.2 us
  local copies, waits for them, and re-layouts: 28.7 us -> 37.4 us
  blocking collectives: 177 us -> 182 us
    all_gather x1, blocking collectives: 11.9 us -> 99.2 us  [local(): lax.all_gather(variate_ids, 'mp', axis=0, tiled=True)]
    all_gather x1, blocking collectives: 107 us -> 27.9 us  [local(): down_full = lax.all_gather(down_weight, 'mp', axis=0, tiled=True)]
    all_gather x1, waiting for transfers between devices: 41.2 us -> 24.6 us  [local(): lax.all_gather(wide_columns, 'dp', axis=1, tiled=True)]
    reshape x0 -> x1, local copies, waits for them, and re-layouts: none -> 8.19 us  [results_raise(): near = jnp.concatenate(frame_out, axis=d0)]
    dot_general x1, matrix products: 10.2 us -> 4.32 us  [local(): jnp.dot(hidden, clear_regions_for(down_full), preferred_element_type=jnp....]
    all_to_all x1, waiting for transfers between devices: 18.6 us -> 13.5 us  [local(): lax.all_to_all(attended, 'mp', split_axis=0, concat_axis=1, tiled=True)]
    dot_general x1, matrix products: 13.2 us -> 9.27 us  [local(): jnp.einsum('rc,jcf->jrf', columns, lax.all_gather(ffn_columns, 'dp', axis...]
    all_gather x1, blocking collectives: 18.9 us -> 15 us  [local(): out_rows = lax.all_gather(out_weight, 'mp', axis=0, tiled=True)]
  transfers between devices with their start and end apart: 7 -> 7, of which waited for: 3 -> 2; matrix products, arithmetic and copies ran while one was open for 24% -> 23% of each run, Pallas kernels for 0% -> 0%
where the time goes in v1:
time: 336 us; the launch traced here: 335 us
  blocking collectives  182 us (54%)
  matrix products  48.2 us (14%)
  waiting for transfers between devices  38.3 us (11%)
  local copies, waits for them, and re-layouts  37.4 us (11%)
  between operations  13.4 us (4%)
  starting transfers between devices  8.91 us (3%)
  other arithmetic  6.94 us (2%)
    all_gather x1, blocking collectives, local(): lax.all_gather(variate_ids, 'mp', axis=0, tiled=True)  99.2 us
    all_gather x1, blocking collectives, local(): wide_columns = lax.all_gather(qkv_weight, 'mp', axis=2, tiled=True)  27.9 us
    all_gather x1, blocking collectives, local(): down_full = lax.all_gather(down_weight, 'mp', axis=0, tiled=True)  27.9 us
    all_gather x1, waiting for transfers between devices, local(): lax.all_gather(wide_columns, 'dp', axis=1, tiled=True)  24.6 us
    dot_general x4, matrix products, one_sequence(): jnp.einsum('hqk,khd->qhd', weights, vs, preferred_element_type=jnp.float32)  16.9 us
    all_gather x1, blocking collectives, local(): out_rows = lax.all_gather(out_weight, 'mp', axis=0, tiled=True)  15 us
    all_to_all x1, waiting for transfers between devices, local(): lax.all_to_all(attended, 'mp', split_axis=0, concat_axis=1, tiled=True)  13.5 us
    all_gather x1, blocking collectives, local(): lax.all_gather(sample_ids, 'mp', axis=0, tiled=True)  12.1 us
  transfers between devices with their start and end apart: 7, of which 2 were waited for; matrix products, arithmetic and copies ran while one was open for 23% of the time, Pallas kernels for 0%

profile of v1, /device:TPU:0, one launch (start us, length us, event | category | flops | bytes accessed | tf_op | source)
XLA Modules:
  0.0 335.3 jit_solution(1875265429823034141)
XLA Ops:
  6.5 2.1 copy.51
  8.8 27.9 %all_gather.33 = bf16[3,128,1024]{2,1,0:T(8,128)(2,1)} all-gather(bf16[3,128,256]{2,1,0:T(8,128)(2,1)} %param.14), channel_id=1, replica_groups=mesh['dp'=8,'mp'=4] {'mp'}, dimensions={2}, use_global_device_ids=true | all-gather | bytes 983040 | tf_op jit(solution)/shard_map/all_gather | solution.py:95
  36.7 27.9 %all_gather.41 = bf16[2816,128]{1,0:T(8,128)(2,1)} all-gather(bf16[704,128]{1,0:T(8,128)(2,1)} %param.18), channel_id=1, replica_groups=mesh['dp'=8,'mp'=4] {'mp'}, dimensions={0}, use_global_device_ids=true | all-gather | bytes 901120 | tf_op jit(solution)/shard_map/all_gather | solution.py:134
  64.7 15.0 %all_gather.37 = bf16[1024,128]{1,0:T(8,128)(2,1)} all-gather(bf16[256,128]{1,0:T(8,128)(2,1)S(1)} %copy-done.4), channel_id=1, replica_groups=mesh['dp'=8,'mp'=4] {'mp'}, dimensions={0}, use_global_device_ids=true | all-gather | bytes 327680 | tf_op jit(solution)/shard_map/all_gather | solution.py:117
  79.8 4.9 %copy.52 = bf16[2,128,2816]{2,1,0:T(8,128)(2,1)} copy(bf16[2,128,2816]{1,0,2:T(2,128)(2,1)} %all-gather.13.cloned.1.call-done) | data formatting | bytes 2883584 | tf_op jit(solution)/shard_map/all_gather | solution.py:125
  84.8 0.3 fusion.56
  85.1 0.3 multiply_cosine_fusion
  85.4 24.6 %all-gather.9.cloned.1.call-done = bf16[3,1024,1024]{2,1,0:T(8,128)(2,1)} async-done(((bf16[3,128,1024]{2,1,0:T(8,128)(2,1)}), bf16[3,1024,1024]{2,1,0:T(8,128)(2,1)}) %all-gather.9.cloned.1.call-update) | async-done | bytes 6291472 | tf_op jit(solution)/shard_map/all_gather | solution.py:100
  110.1 5.7 %convolution_bitcast_fusion.1 = f32[3,512,1024]{2,1,0:T(8,128)S(1)} fusion(bf16[3,1024,1024]{2,1,0:T(8,128)(2,1)} %all-gather.9.cloned.1.call-done, bf16[512,1024]{1,0:T(8,128)(2,1)S(1)} %copy-done.2, f32[1024]{0:T(1024)S(1)} %bitcast.125, f32[512]{0:T(512)S(1)} %add_rsqrt_fusion.1), kind=kOutput, calls=%fused_computation.53 | convolution fusion | flops 3223322624 | bytes 13637632 | tf_op jit(solution)/shard_map/rc,jcd->jrd/dot_general | solution.py:97
  115.8 1.1 slice.103
  116.9 2.4 fusion.80
  119.3 2.0 copy.45
  121.3 3.0 copy.46
  124.2 2.3 subtract_convert_fusion.1
  126.5 0.1 pad_maximum_fusion.1
  126.7 1.3 copy.47
  128.0 1.3 copy.48
  129.3 2.2 pad_maximum_fusion
  131.5 5.8 %copy.49 = bf16[3,512,1024]{1,0,2:T(4,128)(2,1)} copy(bf16[3,512,1024]{2,1,0:T(8,128)(2,1)S(1)} %pad_maximum_fusion) | data formatting | bytes 6291456 | tf_op jit(solution)/shard_map/stack | solution.py:107
  137.3 5.0 %all-to-all-start = ((bf16[3,512,1024]{1,0,2:T(4,128)(2,1)}), bf16[3,512,1024]{1,0,2:T(4,128)(2,1)}, u32[]{:S(2)}, u32[]{:S(2)}) async-start(bf16[3,512,1024]{1,0,2:T(4,128)(2,1)} %copy.49), calls=%async_computation | async-start | bytes 8388608 | tf_op jit(solution)/shard_map/all_to_all | solution.py:106
  142.3 99.2 %all-gather.2 = s32[4,1,512]{2,1,0:T(1,128)S(1)} all-gather(s32[1,1,512]{2,1,0:T(1,128)S(1)} %bitcast.126), channel_id=1, replica_groups=mesh['dp'=8,'mp'=4] {'mp'}, dimensions={0}, use_global_device_ids=true | all-gather | bytes 10240 | tf_op jit(solution)/shard_map/all_gather | solution.py:111
  241.5 12.1 %all-gather.1 = s32[4,1,512]{2,1,0:T(1,128)S(1)} all-gather(s32[1,1,512]{2,1,0:T(1,128)S(1)} %bitcast.127), channel_id=1, replica_groups=mesh['dp'=8,'mp'=4] {'mp'}, dimensions={0}, use_global_device_ids=true | all-gather | bytes 10240 | tf_op jit(solution)/shard_map/all_gather | solution.py:110
  253.7 3.0 copy.50
  256.7 1.2 fusion.81
  257.9 27.1 %while.10 = (s32[]{:T(128)}, bf16[4,512,4,64]{1,3,2,0:T(8,128)(2,1)}, bf16[4,512,4,64]{1,3,2,0:T(8,128)(2,1)}, s32[4,512]{1,0:T(4,128)S(1)}, bf16[4,512,4,64]{1,...) while((s32[]{:T(128)}, ...), condition=%wide.region_4.5_spmd, body=%wide.region_1.4_spmd.sunk | while | flops 416943104 | bytes 3179681 | solution.py:66
  257.9 0.2 broadcast_compare_fusion.4
  258.1 0.2 broadcast_compare_fusion.5
  258.3 2.1 fusion.100
  260.4 4.2 %fusion.101 = bf16[4,512,4,64]{1,3,2,0:T(8,128)(2,1)} fusion(bf16[4,512,4,64]{1,3,2,0:T(8,128)(2,1)} %get-tuple-element.154, s32[]{:T(128)} %get-tuple-element.153, f32[4,512]{1,0:T(4,128)S(1)} %fusion.100, bf16[4,512,4,64]{1,3,2,0:T(8,128)(2,1)} %get-tuple-element.164, f32[4]{0:T(128)S(1)} %get-tuple-element.140, f32[4]{0:T(128)S(1)} %get-tuple-element.141, ...), kind=kOutput, calls=%fused_computation.14.clone.1 | convolution fusion | flops 275909120 | bytes 1584128 | tf_op jit(solution)/shard_map/while/body/eval_jaxpr/hqk,khd->qhd/dot_general | solution.py:61
  264.7 0.2 broadcast_compare_fusion.4
  264.9 0.2 broadcast_compare_fusion.5
  265.1 2.1 fusion.100
  267.2 4.2 %fusion.101 = bf16[4,512,4,64]{1,3,2,0:T(8,128)(2,1)} fusion(bf16[4,512,4,64]{1,3,2,0:T(8,128)(2,1)} %get-tuple-element.154, s32[]{:T(128)} %get-tuple-element.153, f32[4,512]{1,0:T(4,128)S(1)} %fusion.100, bf16[4,512,4,64]{1,3,2,0:T(8,128)(2,1)} %get-tuple-element.164, f32[4]{0:T(128)S(1)} %get-tuple-element.140, f32[4]{0:T(128)S(1)} %get-tuple-element.141, ...), kind=kOutput, calls=%fused_computation.14.clone.1 | convolution fusion | flops 275909120 | bytes 1584128 | tf_op jit(solution)/shard_map/while/body/eval_jaxpr/hqk,khd->qhd/dot_general | solution.py:61
  271.4 0.2 broadcast_compare_fusion.4
  271.7 0.2 broadcast_compare_fusion.5
  271.9 2.1 fusion.100
  274.0 4.2 %fusion.101 = bf16[4,512,4,64]{1,3,2,0:T(8,128)(2,1)} fusion(bf16[4,512,4,64]{1,3,2,0:T(8,128)(2,1)} %get-tuple-element.154, s32[]{:T(128)} %get-tuple-element.153, f32[4,512]{1,0:T(4,128)S(1)} %fusion.100, bf16[4,512,4,64]{1,3,2,0:T(8,128)(2,1)} %get-tuple-element.164, f32[4]{0:T(128)S(1)} %get-tuple-element.140, f32[4]{0:T(128)S(1)} %get-tuple-element.141, ...), kind=kOutput, calls=%fused_computation.14.clone.1 | convolution fusion | flops 275909120 | bytes 1584128 | tf_op jit(solution)/shard_map/while/body/eval_jaxpr/hqk,khd->qhd/dot_general | solution.py:61
  278.2 0.2 broadcast_compare_fusion.4
  278.4 0.2 broadcast_compare_fusion.5
  278.7 2.1 fusion.100
  280.8 4.2 %fusion.101 = bf16[4,512,4,64]{1,3,2,0:T(8,128)(2,1)} fusion(bf16[4,512,4,64]{1,3,2,0:T(8,128)(2,1)} %get-tuple-element.154, s32[]{:T(128)} %get-tuple-element.153, f32[4,512]{1,0:T(4,128)S(1)} %fusion.100, bf16[4,512,4,64]{1,3,2,0:T(8,128)(2,1)} %get-tuple-element.164, f32[4]{0:T(128)S(1)} %get-tuple-element.140, f32[4]{0:T(128)S(1)} %get-tuple-element.141, ...), kind=kOutput, calls=%fused_computation.14.clone.1 | convolution fusion | flops 275909120 | bytes 1584128 | tf_op jit(solution)/shard_map/while/body/eval_jaxpr/hqk,khd->qhd/dot_general | solution.py:61
  285.0 3.7 %all-to-all-start.1 = ((bf16[4,512,256]{1,2,0:T(8,128)(2,1)}), bf16[4,512,256]{1,2,0:T(8,128)(2,1)S(1)}, u32[]{:S(2)}, u32[]{:S(2)}) async-start(bf16[4,512,256]{1,2,0:T(8,128)(2,1)} %bitcast.24), calls=%async_computation.1 | async-start | bytes 2097152 | tf_op jit(solution)/shard_map/all_to_all | solution.py:116
  288.8 8.2 %copy.53 = bf16[2816,8,128]{0,2,1:T(8,128)(2,1)} copy(bf16[2816,8,128]{2,0,1:T(8,128)(2,1)} %bitcast.110) | data formatting | bytes 11534336 | tf_op jit(solution)/shard_map/reshape | solution.py:13
  297.0 13.5 %all-to-all-done.1 = bf16[4,512,256]{1,2,0:T(8,128)(2,1)S(1)} async-done(((bf16[4,512,256]{1,2,0:T(8,128)(2,1)}), bf16[4,512,256]{1,2,0:T(8,128)(2,1)S(1)}, u32[]{:S(2)}, u32[]{:S(2)}) %all-to-all-start.1) | async-done | bytes 1048608 | tf_op jit(solution)/shard_map/all_to_all | solution.py:116
  310.5 1.0 copy-done.3
  311.4 3.7 %fusion.60 = (f32[512]{0:T(512)S(1)}, bf16[512,1024]{1,0:T(8,128)(2,1)S(1)}) fusion(bf16[512,1024]{0,1:T(8,128)(2,1)} %bitcast.116, bf16[1024,1024]{1,0:T(8,128)(2,1)} %all-gather.11.cloned.1.call-done, bf16[512,1024]{1,0:T(8,128)(2,1)} %param.12), kind=kOutput, calls=%fused_computation.58 | convolution fusion | flops 1076887040 | bytes 5244928 | tf_op jit(solution)/shard_map/dot_general | solution.py:118
  315.2 9.3 %convolution_bitcast_fusion = f32[2,512,2816]{2,1,0:T(8,128)S(1)} fusion(bf16[2,1024,2816]{2,1,0:T(8,128)(2,1)} %all-gather.15.cloned.1.call-done, bf16[512,1024]{1,0:T(8,128)(2,1)S(1)} %get-tuple-element.84, f32[1024]{0:T(1024)S(1)} %bitcast.122, f32[512]{0:T(512)S(1)} %add_rsqrt_fusion), kind=kOutput, calls=%fused_computation.41 | convolution fusion | flops 5907677184 | bytes 24123392 | tf_op jit(solution)/shard_map/rc,jcf->jrf/dot_general | solution.py:127
  324.5 4.3 %fusion.63 = bf16[512,1024]{1,0:T(8,128)(2,1)} fusion(bf16[512,1024]{1,0:T(8,128)(2,1)S(1)} %get-tuple-element.84, bf16[2816,1024]{0,1:T(8,128)(2,1)S(1)} %bitcast.113, f32[2,512,2816]{2,1,0:T(8,128)S(1)} %convolution_bitcast_fusion), kind=kOutput, calls=%fused_computation.61 | convolution fusion | flops 2963013632 | bytes 19398656 | tf_op jit(solution)/shard_map/dot_general | solution.py:135
  (54 shorter events, 0.5 us)
Async XLA Ops:
  6.5 247.1 %copy-start = (f32[2,16]{1,0:T(2,128)S(1)}, f32[2,16]{1,0:T(2,128)}, u32[]{:S(2)}) copy-start(f32[2,16]{1,0:T(2,128)} %param.16) | copy-start | bytes 388
  6.5 58.1 %copy-start.4 = (bf16[256,128]{1,0:T(8,128)(2,1)S(1)}, bf16[256,128]{1,0:T(8,128)(2,1)}, u32[]{:S(2)}) copy-start(bf16[256,128]{1,0:T(8,128)(2,1)} %param.15) | copy-start | bytes 196612
  6.5 73.3 %all-gather.13.cloned.1.call-start = ((), (), s32[]{:S(2)}) async-start(), calls=%async_computation.4 | async-start | bytes 1802240 | tf_op jit(solution)/shard_map/all_gather | solution.py:125
  8.7 76.1 %copy-start.8 = (s32[512]{0:T(512)S(1)}, s32[512]{0:T(512)}, u32[]{:S(2)}) copy-start(s32[512]{0:T(512)} %param.21) | copy-start | bytes 6148
  8.7 76.1 %copy-start.2 = (bf16[512,1024]{1,0:T(8,128)(2,1)S(1)}, bf16[512,1024]{1,0:T(8,128)(2,1)}, u32[]{:S(2)}) copy-start(bf16[512,1024]{1,0:T(8,128)(2,1)} %param.12) | copy-start | bytes 3145732
  8.7 101.3 %all-gather.9.cloned.1.call-start = ((), (), s32[]{:S(2)}) async-start(), calls=%async_computation.2 | async-start | bytes 7077888 | tf_op jit(solution)/shard_map/all_gather | solution.py:100
  36.7 48.4 %copy-start.5 = (f32[2,1024]{1,0:T(2,128)S(1)}, f32[2,1024]{1,0:T(2,128)}, u32[]{:S(2)}) copy-start(f32[2,1024]{1,0:T(2,128)} %param.13) | copy-start | bytes 24580
  36.7 252.1 %all-gather.17.cloned.1.call-start = ((), (), s32[]{:S(2)}) async-start(), calls=%async_computation.6 | async-start | bytes 6488064 | tf_op jit(solution)/shard_map/all_gather | solution.py:12
  64.6 232.3 %all-gather.11.cloned.1.call-start = ((), (), s32[]{:S(2)}) async-start(), calls=%async_computation.3 | async-start | bytes 2359296 | tf_op jit(solution)/shard_map/all_gather | solution.py:120
  79.8 235.4 %all-gather.15.cloned.1.call-start = ((), (), s32[]{:S(2)}) async-start(), calls=%async_computation.5 | async-start | bytes 12976128 | tf_op jit(solution)/shard_map/all_gather | solution.py:130
  137.3 5.0 %copy-start.6 = (s32[512]{0:T(512)S(1)}, s32[512]{0:T(512)}, u32[]{:S(2)}) copy-start(s32[512]{0:T(512)} %param.20) | copy-start | bytes 6148
  137.3 104.2 %copy-start.7 = (s32[512]{0:T(512)S(1)}, s32[512]{0:T(512)}, u32[]{:S(2)}) copy-start(s32[512]{0:T(512)} %param.19) | copy-start | bytes 6148
  137.3 116.4 %all-to-all-start = ((bf16[3,512,1024]{1,0,2:T(4,128)(2,1)}), bf16[3,512,1024]{1,0,2:T(4,128)(2,1)}, u32[]{:S(2)}, u32[]{:S(2)}) async-start(bf16[3,512,1024]{1,0,2:T(4,128)(2,1)} %copy.49), calls=%async_computation | async-start | bytes 8388608 | tf_op jit(solution)/shard_map/all_to_all | solution.py:106
  285.0 25.5 %all-to-all-start.1 = ((bf16[4,512,256]{1,2,0:T(8,128)(2,1)}), bf16[4,512,256]{1,2,0:T(8,128)(2,1)S(1)}, u32[]{:S(2)}, u32[]{:S(2)}) async-start(bf16[4,512,256]{1,2,0:T(8,128)(2,1)} %bitcast.24), calls=%async_computation.1 | async-start | bytes 2097152 | tf_op jit(solution)/shard_map/all_to_all | solution.py:116
  310.5 1.0 copy-start.3
  311.4 13.0 %slice-start = ((s8[5767168]{0:T(1024)(128)(4,1)}), s8[1572864]{0:T(1024)(128)(4,1)S(1)}, s32[]{:S(2)}) async-start(s8[5767168]{0:T(1024)(128)(4,1)} %bitcast.111), calls=%async_computation.7 | async-start | bytes 3145728
  315.2 9.3 %slice-start.1 = ((s8[5767168]{0:T(1024)(128)(4,1)}), s8[4194304]{0:T(1024)(128)(4,1)S(1)}, s32[]{:S(2)}) async-start(s8[5767168]{0:T(1024)(128)(4,1)} %bitcast.111), calls=%async_computation.8 | async-start | bytes 8388608
  324.5 4.3 %copy-start.1 = (f32[2,16]{1,0:T(2,128)S(1)}, f32[2,16]{1,0:T(2,128)}, u32[]{:S(2)}) copy-start(f32[2,16]{1,0:T(2,128)} %param.16) | copy-start | bytes 388
Sparse Core Ops, SparseCore 0:
  8.9 54.3 all-gather.12
  65.2 44.7 all-gather.8
  111.9 43.1 all-gather.16
  156.9 28.0 all-gather.10
  186.8 67.5 all-gather.14
